TPU v7x, 512 devices: a whole 4x4x16 slice. The times are simulated.
512 devices in a mesh: rows: 128 (over y_lo, x, z), cols: 4 (over y_hi, core).
Axes of the slice: x: 4, y: 4 (y_hi: 2, y_lo: 2; y = y_hi * 2 + y_lo), z: 16, core: 2. Of those that a mesh axis runs over, the one named last changes fastest.
Arguments:
- grad_out: bfloat16 [512, 512, 192], P(('rows', 'cols')), may hold values from -6 to 6
- inputs: bfloat16 [1024, 1024, 192], P('rows', 'cols'), may hold values from -6 to 6
- weight: bfloat16 [3, 3, 192, 192], replicated, may hold values from -0.15625 to 0.15625
Outputs:
- input_grad: bfloat16 [1024, 1024, 192], P('rows', 'cols')
- filter_grad: float32 [3, 3, 192, 192], replicated
All inputs are finite; a program needn't handle non-finite values.
Results may differ from a plain program's by a relative error of at most 0.0028.
Values may be sent and summed in bfloat16 or wider, within the bound.
No kernel may reach another device: no remote copies, remote signals or barrier semaphores. Data moves between devices by JAX's collectives and lax.ppermute only.
A program may use at most 64 MiB of HBM per device.

v0:
```python
import functools
import math

import jax
import jax.numpy as jnp
from jax import lax
from jax.experimental import pallas as pl
from jax.experimental.pallas import tpu as pltpu
from jax.sharding import Mesh
from jax.sharding import PartitionSpec as P


AXES = ("r0", "r1", "z1", "z0", "c0", "c1")
ROWS = ("r0", "r1", "z1", "z0")
COLS = ("c0", "c1")
NEAR = ("r0", "r1", "z0", "c0")
FAR = "z1"
CORE = "c1"
BF = jnp.bfloat16
F32 = jnp.float32
LANES = 128
TOTAL = 3072
NT = (((1,), (1,)), ((), ()))
TN = (((0,), (0,)), ((), ()))
STEPS = 32256.0
SMALLEST = 2.0**-126
NN = (((1,), (0,)), ((), ()))


def mm(a, b, dims):
    return lax.dot_general(a, b, dims, preferred_element_type=F32)


def call(body, outs, flops, moved):
    return pl.pallas_call(
        body,
        out_shape=outs,
        cost_estimate=pl.CostEstimate(flops=flops, bytes_accessed=moved, transcendentals=0),
        compiler_params=pltpu.CompilerParams(vmem_limit_bytes=24 * 1024 * 1024),
    )


def split_matrix(width):
    half = width // 2
    q = lax.broadcasted_iota(jnp.int32, (width, width), 0)
    n = lax.broadcasted_iota(jnp.int32, (width, width), 1)
    source = jnp.where(n < half, 2 * n, 2 * (n - half) + 1)
    return jnp.where(q == source, 1.0, 0.0).astype(BF)


def send_body(grad_ref, lines_ref, out_ref, row_ref, grad, line, edges, in_sem, out_sem):
    chans, width = grad_ref.shape
    blocks = out_ref.shape[0]
    block = width // blocks
    take_grad = pltpu.make_async_copy(grad_ref, grad, in_sem.at[0])
    take_line = pltpu.make_async_copy(lines_ref.at[lines_ref.shape[0] - 1], line, in_sem.at[1])
    take_grad.start()
    take_line.start()
    r = lax.broadcasted_iota(jnp.int32, (8, width), 0)
    q = lax.broadcasted_iota(jnp.int32, (8, width), 1)
    pick = jnp.where(q == (r + 1) * block, 1.0, 0.0).astype(BF)
    take_grad.wait()
    puts = []
    for d in range(blocks):
        puts.append(
            pltpu.make_async_copy(
                grad.at[:, pl.ds(d * block, block)], out_ref.at[d, pl.ds(0, chans), :], out_sem.at[d]
            )
        )
    puts.append(pltpu.make_async_copy(line, row_ref, out_sem.at[blocks]))
    for put in puts[:blocks]:
        put.start()
    edge = mm(pick, grad[...], NT)
    head = edge[:, :LANES]
    tail = jnp.concatenate([edge[:, LANES:], jnp.zeros((8, 2 * LANES - chans), F32)], axis=1)
    take_line.wait()
    puts[blocks].start()
    for d in range(blocks):
        edges[d] = jnp.concatenate([head[d : d + 1], tail[d : d + 1], jnp.zeros((6, LANES), F32)], axis=0).astype(BF)
    puts.append(pltpu.make_async_copy(edges, out_ref.at[:, pl.ds(chans, 8), :], out_sem.at[blocks + 1]))
    puts[-1].start()
    for put in puts:
        put.wait()


def split_body(lines_ref, split_ref):
    rows, chans, width = lines_ref.shape
    flat = lines_ref[...].reshape(rows * chans, width)
    split_ref[...] = mm(flat, split_matrix(width), NN).astype(BF).reshape(rows, chans, width)


def shifted(grads, edges):
    q = lax.broadcasted_iota(jnp.int32, (LANES, LANES), 0)
    n = lax.broadcasted_iota(jnp.int32, (LANES, LANES), 1)
    move = jnp.where(q == n + 1, 1.0, 0.0).astype(BF)
    r = lax.broadcasted_iota(jnp.int32, (8, LANES), 0)
    lane = lax.broadcasted_iota(jnp.int32, (8, LANES), 1)
    out = []
    for k, block in enumerate(grads):
        place = jnp.where((r == k) & (lane == LANES - 1), 1.0, 0.0).astype(BF)
        out.append((mm(block, move, NN) + mm(edges, place, TN)).astype(BF))
    return out


def edges_of(blocks, chans):
    rows = [jnp.concatenate([b[chans : chans + 1, :], b[chans + 1 : chans + 2, : chans - LANES]], axis=1) for b in blocks]
    rows.append(jnp.zeros((8 - len(rows), chans), BF))
    return jnp.concatenate(rows, axis=0)


def filter_body(got_ref, split_ref, above_ref, out_ref, pair_ref):
    rows, chans, width = split_ref.shape
    half = rows // 2
    mine = lax.axis_index(CORE)
    top = mm(above_ref[...], split_matrix(width), NN).astype(BF)
    blocks = [got_ref[k] for k in range(half)]
    grads = [b[:chans, :] for b in blocks]
    moved = shifted(grads, edges_of(blocks, chans))
    for k in range(half):
        pair_ref[k, 0] = grads[k]
        pair_ref[k, 1] = moved[k]
    spare = jnp.zeros((2 * LANES - chans, half * LANES), BF)
    here = jnp.concatenate([jnp.concatenate(grads, axis=1), spare], axis=0)
    right = jnp.concatenate([jnp.concatenate(moved, axis=1), spare], axis=0)

    def line(p, odd):
        lanes = slice(LANES, 2 * LANES) if odd else slice(0, LANES)
        return top[:, lanes] if p < 0 else split_ref[p, :, lanes]

    own = out_ref.shape[1]

    def put(base, value):
        count = value.shape[0]
        for core in range(2):
            low, high = max(base, core * own), min(base + count, (core + 1) * own)
            if low < high:
                out_ref[mine ^ core, low - core * own : high - core * own, :] = value[low - base : high - base]

    step = chans + chans // 2
    for a in range(3):
        for b in range(3):
            left = jnp.concatenate([line(2 * k + a - 1, b != 1) for k in range(half)], axis=1)
            term = mm(left, right if b == 0 else here, NT)
            base = (3 * a + b) * step
            far = term[:, LANES:]
            put(base, term[:, :LANES])
            put(base + chans, far[: chans // 2] + pltpu.roll(far[chans // 2 :], LANES // 2, 1))
    put(9 * step, jnp.zeros((TOTAL - 9 * step, LANES), F32))


def pair_body(mine_ref, other_ref, out_ref):
    out_ref[...] = (mine_ref[0] + other_ref[...]).astype(BF)


def coded(value, top):
    count = jnp.floor(jnp.abs(value) * (STEPS / top) + 0.5)
    power = jnp.floor(count * (1.0 / 128.0))
    rest = count - 128.0 * power
    code = (1.0 + rest * (1.0 / 128.0)) * SMALLEST
    power = power.astype(jnp.int32)
    for bit in (0, 1, 2, 3, 4, 5, 6, 7, 7):
        code = jnp.where((power & (1 << bit)) != 0, code * 2.0 ** min(1 << bit, 64), code)
    return jnp.where(value < 0, -code, code).astype(BF)


def decoded(code, top):
    code = code.astype(F32)
    size = jnp.abs(code)
    big = size >= 4.0
    power = jnp.where(big, 128.0, 0.0)
    for _ in range(2):
        size = jnp.where(big, size * 2.0**-64, size)
    for bit in range(6, -1, -1):
        span = float(1 << bit)
        big = size >= SMALLEST * 2.0**span
        size = jnp.where(big, size * 2.0**-span, size)
        power = jnp.where(big, power + span, power)
    count = 128.0 * power + (size * (1.0 / SMALLEST) - 1.0) * 128.0
    return jnp.where(code < 0, -count, count) * (top * (1.0 / STEPS))


def near_body(in_ref, out_ref):
    total = jnp.sum(in_ref[...].astype(F32), axis=0)
    chunk = total.shape[0]
    top = jnp.max(jnp.max(jnp.abs(total), axis=0, keepdims=True), axis=1, keepdims=True)
    top = jnp.maximum(top * 1.0078125, 1e-30).astype(BF)
    code = coded(total, top.astype(F32))
    head = jnp.broadcast_to(top, (8, LANES))
    for k in range(out_ref.shape[0]):
        out_ref[k, :chunk, :] = code
        out_ref[k, chunk:, :] = head


def far_body(in_ref, out_ref):
    chunk = out_ref.shape[1]
    total = None
    for k in range(in_ref.shape[0]):
        top = in_ref[k, chunk:, :].astype(F32)[:1]
        term = decoded(in_ref[k, :chunk, :], top)
        total = term if total is None else total + term
    out_ref[...] = jnp.broadcast_to(total.astype(BF)[None], out_ref.shape)


def merge_matrix(width):
    half = width // 2
    n = lax.broadcasted_iota(jnp.int32, (width, width), 0)
    q = lax.broadcasted_iota(jnp.int32, (width, width), 1)
    return jnp.where(q == jnp.where(n < half, 2 * n, 2 * (n - half) + 1), 1.0, 0.0).astype(BF)


def merged(even, odd, merge):
    return mm(jnp.concatenate([even, odd], axis=1).astype(BF), merge, NN).astype(BF)


def input_body(pair_ref, weight_ref, out_ref, part_ref):
    rows, chans, width = out_ref.shape
    half = rows // 2
    grads = [pair_ref[k, 0] for k in range(half)]
    moved = [pair_ref[k, 1] for k in range(half)]
    here = jnp.concatenate(grads, axis=1)
    right = jnp.concatenate(moved, axis=1)
    here_down = jnp.concatenate(grads[1:], axis=1)
    right_down = jnp.concatenate(moved[1:], axis=1)

    def tap(a, b, g):
        return mm(weight_ref[a, b], g, NN)

    even_even = tap(1, 1, here)
    even_odd = tap(1, 2, here) + tap(1, 0, right)
    odd_even = tap(2, 1, here)
    odd_odd = tap(2, 2, here) + tap(2, 0, right)
    odd_even_down = tap(0, 1, here_down)
    odd_odd_down = tap(0, 2, here_down) + tap(0, 0, right_down)
    merge = merge_matrix(width)
    for k in range(half):
        cut = slice(k * LANES, (k + 1) * LANES)
        out_ref[2 * k] = merged(even_even[:, cut], even_odd[:, cut], merge)
        if k < half - 1:
            out_ref[2 * k + 1] = merged(
                odd_even[:, cut] + odd_even_down[:, cut], odd_odd[:, cut] + odd_odd_down[:, cut], merge
            )
        else:
            part_ref[0] = odd_even[:, cut]
            part_ref[1] = odd_odd[:, cut]
            out_ref[2 * k + 1] = jnp.zeros((chans, width), BF)


def last_body(scale, in_ref, below_ref, weight_ref, part_ref, _, out_ref, grad_ref, whole, line, sem):
    chans = out_ref.shape[-1]
    rows, _, width = grad_ref.shape
    step = chans + chans // 2
    copies = []

    def tap(t):
        base = t * step
        near = in_ref[base : base + chans, :].astype(F32) * scale
        far = in_ref[base + chans : base + step, :].astype(F32) * scale
        whole[t, :, :LANES] = near
        whole[t, : chans // 2, LANES:] = far[:, : LANES // 2]
        whole[t, chans // 2 :, LANES:] = pltpu.roll(far, LANES // 2, 1)[:, : LANES // 2]
        copies.append(pltpu.make_async_copy(whole.at[t], out_ref.at[t], sem.at[t]))
        copies[-1].start()

    for t in range(3):
        tap(t)
    block = below_ref[...]
    here = block[:chans, :]
    right = shifted([here], edges_of([block], chans))[0]
    even = part_ref[0] + mm(weight_ref[0, 1], here, NN)
    odd = part_ref[1] + mm(weight_ref[0, 2], here, NN) + mm(weight_ref[0, 0], right, NN)
    line[...] = merged(even, odd, merge_matrix(width))
    copies.append(pltpu.make_async_copy(line, grad_ref.at[rows - 1], sem.at[9]))
    copies[-1].start()
    for t in range(3, 9):
        tap(t)
    for copy in copies:
        copy.wait()


def shape(dims, dtype):
    return jax.ShapeDtypeStruct(dims, dtype)


def moved_rows(x, by):
    devices = lax.axis_size(ROWS)
    pairs = [(i, i + by) for i in range(devices) if 0 <= i + by < devices]
    return lax.ppermute(x, ROWS, pairs)


def swap(x, axes):
    return lax.all_to_all(x, axes, split_axis=0, concat_axis=0, tiled=True)


def step(grad_out, inputs, weight):
    chans = weight.shape[2]
    rows, cols = inputs.shape[:2]
    half = rows // 2
    near, far = lax.axis_size(NEAR), lax.axis_size(FAR)
    own = TOTAL // lax.axis_size(CORE)
    chunk = own // near
    positions = half * lax.axis_size(ROWS) * (cols // 2) * lax.axis_size(COLS)
    grad = jnp.transpose(grad_out, (0, 2, 1))[0]
    lines = jnp.transpose(inputs, (0, 2, 1))

    stored = pl.BlockSpec(memory_space=pltpu.HBM)
    local = pl.BlockSpec(memory_space=pltpu.VMEM)
    blocks = lax.axis_size(COLS)
    sent, last = pl.pallas_call(
        send_body,
        in_specs=[stored, stored],
        out_specs=[stored, stored],
        out_shape=[shape((blocks, chans + 8, LANES), BF), shape((chans, cols), BF)],
        scratch_shapes=[
            pltpu.VMEM(grad.shape, BF),
            pltpu.VMEM((chans, cols), BF),
            pltpu.VMEM((blocks, 8, LANES), BF),
            pltpu.SemaphoreType.DMA((2,)),
            pltpu.SemaphoreType.DMA((blocks + 2,)),
        ],
        cost_estimate=pl.CostEstimate(flops=10**8, bytes_accessed=5 * 10**5, transcendentals=0),
        compiler_params=pltpu.CompilerParams(vmem_limit_bytes=63000000),
    )(grad, lines)
    got = swap(sent, COLS)
    above = moved_rows(last, 1)
    split = call(split_body, shape((rows, chans, cols), BF), 2 * 10**8, 2 * 10**6)(lines)
    below = moved_rows(got[0], -1)
    terms, pairs = call(
        filter_body,
        (shape((2, own, LANES), F32), shape((half, 2, chans, LANES), BF)),
        10**9,
        4 * 10**6,
    )(got, split, above)
    other = lax.ppermute(terms[1], CORE, [(0, 1), (1, 0)])
    input_grad, odd_part = call(
        input_body, (shape((rows, chans, cols), BF), shape((2, chans, LANES), F32)), 10**9, 2 * 10**6
    )(pairs, weight)
    part = call(pair_body, shape((own, LANES), BF), 10**6, 2 * 10**6)(terms, other)
    part = swap(part.reshape(near, chunk, LANES), NEAR)
    part = call(near_body, shape((far, chunk + 8, LANES), BF), 10**6, 10**6)(part)
    part = lax.all_to_all(part, FAR, 0, 0, tiled=True, axis_index_groups=[[4, 5, 6, 7, 0, 1, 2, 3]])
    part = call(far_body, shape((near, chunk, LANES), BF), 10**6, 10**6)(part)
    part = swap(part, NEAR).reshape(own, LANES)
    whole = lax.all_gather(part, CORE, axis=0, tiled=True)
    filter_grad, input_grad = pl.pallas_call(
        functools.partial(last_body, 1.0 / math.sqrt(positions)),
        out_shape=(shape((9, chans, chans), F32), shape((rows, chans, cols), BF)),
        in_specs=[local, local, local, local, stored],
        out_specs=(stored, stored),
        input_output_aliases={4: 1},
        scratch_shapes=[
            pltpu.VMEM((9, chans, chans), F32),
            pltpu.VMEM((chans, cols), BF),
            pltpu.SemaphoreType.DMA((10,)),
        ],
        cost_estimate=pl.CostEstimate(flops=10**6, bytes_accessed=2 * 10**6, transcendentals=0),
        compiler_params=pltpu.CompilerParams(vmem_limit_bytes=24 * 1024 * 1024),
    )(whole, below, weight, odd_part, input_grad)
    return (jnp.transpose(input_grad, (0, 2, 1)), filter_grad.reshape(3, 3, chans, chans))


def solution(mesh):
    split = Mesh(mesh.devices.reshape(2, 4, 8, 2, 2, 2), AXES)
    return build(split)


def build(split):
    return jax.shard_map(
        step,
        mesh=split,
        in_specs=(P(ROWS + COLS, None, None), P(ROWS, COLS, None), P()),
        out_specs=(P(ROWS, COLS, None), P()),
        check_vma=False,
    )
```

profile of v0, /device:TPU:1, one launch (start us, length us, event | category | flops | bytes accessed | tf_op | source)
XLA Modules:
  0.0 82.9 jit_solution(8813949793252287069)
XLA Ops:
  0.6 0.0 copy-start
  0.6 1.9 %shard_map.50 = (bf16[4,200,128]{2,1,0:T(8,128)(2,1)}, bf16[192,256]{1,0:T(8,128)(2,1)}) custom-call(bf16[192,512]{1,0:T(8,128)(2,1)} %bitcast.17, bf16[8,192,256]{2,1,0:T(8,128)(2,1)} %bitcast.12), custom_call_target="tpu_custom_call" | custom-call | flops 100000000 | bytes 500000 | tf_op jit(solution)/shard_map/pallas_call | solution.py:308
  2.5 10.2 %all-to-all-start = ((bf16[4,200,128]{2,1,0:T(8,128)(2,1)}), bf16[4,200,128]{2,1,0:T(8,128)(2,1)S(1)}, u32[]{:S(2)}, u32[]{:S(2)}) async-start(bf16[4,200,128]{2,1,0:T(8,128)(2,1)} %get-tuple-element.10), calls=%async_computation | async-start | bytes 409600 | tf_op jit(solution)/shard_map/all_to_all | solution.py:291
  12.7 1.3 %collective-permute-start = (bf16[192,256]{1,0:T(8,128)(2,1)}, bf16[192,256]{1,0:T(8,128)(2,1)S(1)}, u32[]{:S(2)}, u32[]{:S(2)}) collective-permute-start(bf16[192,256]{1,0:T(8,128)(2,1)} %get-tuple-element.11), channel_id=1, source_target_pairs={{0,4},{4,8},{8,12},{12,16},{16,20},{20,24},{24,28},{28,32},{32,36}... | collective-permute-start | bytes 294920 | tf_op jit(solution)/shard_map/ppermute | solution.py:287
  14.0 0.0 copy-done
  14.0 0.4 shard_map.51.split_ref
  14.4 2.3 %collective-permute-done.above_ref = bf16[192,256]{1,0:T(8,128)(2,1)S(1)} collective-permute-done((bf16[192,256]{1,0:T(8,128)(2,1)}, bf16[192,256]{1,0:T(8,128)(2,1)S(1)}, u32[]{:S(2)}, u32[]{:S(2)}) %collective-permute-start) | collective-permute-done | bytes 98336 | tf_op jit(solution)/shard_map/ppermute | solution.py:287
  16.7 1.7 %all-to-all-done.got_ref = bf16[4,200,128]{2,1,0:T(8,128)(2,1)S(1)} async-done(((bf16[4,200,128]{2,1,0:T(8,128)(2,1)}), bf16[4,200,128]{2,1,0:T(8,128)(2,1)S(1)}, u32[]{:S(2)}, u32[]{:S(2)}) %all-to-all-start) | async-done | bytes 204832 | tf_op jit(solution)/shard_map/all_to_all | solution.py:291
  18.4 1.0 %shard_map.52 = (f32[2,1536,128]{2,1,0:T(8,128)S(1)}, bf16[4,2,192,128]{3,2,1,0:T(8,128)(2,1)S(1)}) custom-call(bf16[4,200,128]{2,1,0:T(8,128)(2,1)S(1)} %all-to-all-done.got_ref, bf16[8,192,256]{2,1,0:T(8,128)(2,1)S(1)} %shard_map.51.split_ref, bf16[192,256]{1,0:T(8,128)(2,1)S(1)} %collective-permute-done.above_ref), custom_call_target="tpu_custom_call" | custom-call | flops 1000000000 | bytes 4000000 | tf_op jit(solution)/shard_map/pallas_call | solution.py:327
  19.3 0.1 slice_bitcast_fusion
  19.4 3.1 %collective-permute-start.1 = (f32[1536,128]{1,0:T(8,128)S(1)}, f32[1536,128]{1,0:T(8,128)S(1)}, u32[]{:S(2)}, u32[]{:S(2)}) collective-permute-start(f32[1536,128]{1,0:T(8,128)S(1)} %slice_bitcast_fusion), channel_id=1, source_target_pairs={{0,1},{1,0},{2,3},{3,2},{4,5},{5,4},{6,7},{7,6},{8,9},{9,8},{10,11... | collective-permute-start | bytes 2359304 | tf_op jit(solution)/shard_map/ppermute | solution.py:333
  22.6 1.9 %collective-permute-done.1.other_ref = f32[1536,128]{1,0:T(8,128)S(1)} collective-permute-done((f32[1536,128]{1,0:T(8,128)S(1)}, f32[1536,128]{1,0:T(8,128)S(1)}, u32[]{:S(2)}, u32[]{:S(2)}) %collective-permute-start.1) | collective-permute-done | bytes 786464 | tf_op jit(solution)/shard_map/ppermute | solution.py:333
  24.4 0.1 shard_map.53
  24.5 0.0 copy-start.1
  24.5 21.1 %all_to_all.20.in_ref = bf16[32,48,128]{2,1,0:T(8,128)(2,1)S(1)} all-to-all(bf16[32,48,128]{2,1,0:T(8,128)(2,1)S(1)} %bitcast.14), channel_id=1, replica_groups=mesh['r0'=2,'r1'=4,'z1'=8,'z0'=2,'c0'=2,'c1'=2] {'r0','r1','z0','c0'}, dimensions={0} | all-to-all | bytes 786432 | tf_op jit(solution)/shard_map/all_to_all | solution.py:291
  45.6 0.2 shard_map.54
  45.8 14.8 %all_to_all.21.in_ref = bf16[8,56,128]{2,1,0:T(8,128)(2,1)S(1)} all-to-all(bf16[8,56,128]{2,1,0:T(8,128)(2,1)S(1)} %shard_map.54), channel_id=1, replica_groups={{32,40,48,56,0,8,16,24},{33,41,49,57,1,9,17,25},{34,42,50,58,2,10,18,26..., dimensions={0} | all-to-all | bytes 229376 | tf_op jit(solution)/shard_map/all_to_all | solution.py:340
  60.7 1.1 %shard_map.55 = bf16[32,48,128]{2,1,0:T(8,128)(2,1)} custom-call(bf16[8,56,128]{2,1,0:T(8,128)(2,1)S(1)} %all_to_all.21.in_ref), custom_call_target="tpu_custom_call" | custom-call | flops 1000000 | bytes 1000000 | tf_op jit(solution)/shard_map/pallas_call | solution.py:341
  61.8 3.9 %all-to-all-start.3 = ((bf16[32,48,128]{2,1,0:T(8,128)(2,1)}), bf16[32,48,128]{2,1,0:T(8,128)(2,1)S(1)}, u32[]{:S(2)}, u32[]{:S(2)}) async-start(bf16[32,48,128]{2,1,0:T(8,128)(2,1)} %shard_map.55), calls=%async_computation.3 | async-start | bytes 786432 | tf_op jit(solution)/shard_map/all_to_all | solution.py:291
  65.7 1.3 %collective-permute-start.2 = (bf16[200,128]{1,0:T(8,128)(2,1)S(1)}, bf16[200,128]{1,0:T(8,128)(2,1)S(1)}, u32[]{:S(2)}, u32[]{:S(2)}) collective-permute-start(bf16[200,128]{1,0:T(8,128)(2,1)S(1)} %slice_bitcast_fusion.1), channel_id=1, source_target_pairs={{4,0},{8,4},{12,8},{16,12},{20,16},{24,20},{28,24},{32,28},{36,32}... | collective-permute-start | bytes 153608 | tf_op jit(solution)/shard_map/ppermute | solution.py:287
  67.0 0.0 copy-done.1
  67.0 1.7 %shard_map.56 = (bf16[8,192,256]{2,1,0:T(8,128)(2,1)}, f32[2,192,128]{2,1,0:T(8,128)S(1)}) custom-call(bf16[4,2,192,128]{3,2,1,0:T(8,128)(2,1)S(1)} %get-tuple-element.13.pair_ref, bf16[3,3,192,192]{3,2,1,0:T(8,128)(2,1)S(1)} %copy-done.1), custom_call_target="tpu_custom_call" | custom-call | flops 1000000000 | bytes 2000000 | tf_op jit(solution)/shard_map/pallas_call | solution.py:334
  68.7 6.2 %all-to-all-done.3 = bf16[32,48,128]{2,1,0:T(8,128)(2,1)S(1)} async-done(((bf16[32,48,128]{2,1,0:T(8,128)(2,1)}), bf16[32,48,128]{2,1,0:T(8,128)(2,1)S(1)}, u32[]{:S(2)}, u32[]{:S(2)}) %all-to-all-start.3) | async-done | bytes 393248 | tf_op jit(solution)/shard_map/all_to_all | solution.py:291
  74.8 6.4 %all_gather.3.in_ref = bf16[3072,128]{1,0:T(8,128)(2,1)S(1)} all-gather(bf16[1536,128]{1,0:T(8,128)(2,1)S(1)} %bitcast.15), channel_id=1, replica_groups=mesh['r0'=2,'r1'=4,'z1'=8,'z0'=2,'c0'=2,'c1'=2] {'c1'}, dimensions={0}, use_global_device_ids=true | all-gather | bytes 1179648 | tf_op jit(solution)/shard_map/all_gather | solution.py:343
  81.3 0.0 collective-permute-done.2.below_ref
  81.3 1.6 %shard_map.57 = (f32[9,192,192]{2,1,0:T(8,128)}, bf16[8,192,256]{2,1,0:T(8,128)(2,1)}) custom-call(bf16[3072,128]{1,0:T(8,128)(2,1)S(1)} %all_gather.3.in_ref, bf16[200,128]{1,0:T(8,128)(2,1)S(1)} %collective-permute-done.2.below_ref, bf16[3,3,192,192]{3,2,1,0:T(8,128)(2,1)S(1)} %copy-done.1, ...), custom_call_target="tpu_custom_call", output_to_operand_aliasing={{1}: (4, {})} | custom-call | flops 1000000 | bytes 2000000 | tf_op jit(solution)/shard_map/pallas_call | solution.py:344
  (1 shorter events, 0.0 us)
Async XLA Ops:
  0.6 13.4 %copy-start = (bf16[8,256,192]{1,2,0:T(8,128)(2,1)S(1)}, bf16[8,256,192]{1,2,0:T(8,128)(2,1)}, u32[]{:S(2)}) copy-start(bf16[8,256,192]{1,2,0:T(8,128)(2,1)} %param.4) | copy-start | bytes 2359300
  2.5 15.9 %all-to-all-start = ((bf16[4,200,128]{2,1,0:T(8,128)(2,1)}), bf16[4,200,128]{2,1,0:T(8,128)(2,1)S(1)}, u32[]{:S(2)}, u32[]{:S(2)}) async-start(bf16[4,200,128]{2,1,0:T(8,128)(2,1)} %get-tuple-element.10), calls=%async_computation | async-start | bytes 409600 | tf_op jit(solution)/shard_map/all_to_all | solution.py:291
  12.7 4.0 %collective-permute-start = (bf16[192,256]{1,0:T(8,128)(2,1)}, bf16[192,256]{1,0:T(8,128)(2,1)S(1)}, u32[]{:S(2)}, u32[]{:S(2)}) collective-permute-start(bf16[192,256]{1,0:T(8,128)(2,1)} %get-tuple-element.11), channel_id=1, source_target_pairs={{0,4},{4,8},{8,12},{12,16},{16,20},{20,24},{24,28},{28,32},{32,36}... | collective-permute-start | bytes 294920 | tf_op jit(solution)/shard_map/ppermute | solution.py:287
  19.4 5.0 %collective-permute-start.1 = (f32[1536,128]{1,0:T(8,128)S(1)}, f32[1536,128]{1,0:T(8,128)S(1)}, u32[]{:S(2)}, u32[]{:S(2)}) collective-permute-start(f32[1536,128]{1,0:T(8,128)S(1)} %slice_bitcast_fusion), channel_id=1, source_target_pairs={{0,1},{1,0},{2,3},{3,2},{4,5},{5,4},{6,7},{7,6},{8,9},{9,8},{10,11... | collective-permute-start | bytes 2359304 | tf_op jit(solution)/shard_map/ppermute | solution.py:333
  24.5 42.4 %copy-start.1 = (bf16[3,3,192,192]{3,2,1,0:T(8,128)(2,1)S(1)}, bf16[3,3,192,192]{3,2,1,0:T(8,128)(2,1)}, u32[]{:S(2)}) copy-start(bf16[3,3,192,192]{3,2,1,0:T(8,128)(2,1)} %weight_ref.3) | copy-start | bytes 1990660
  61.8 13.1 %all-to-all-start.3 = ((bf16[32,48,128]{2,1,0:T(8,128)(2,1)}), bf16[32,48,128]{2,1,0:T(8,128)(2,1)S(1)}, u32[]{:S(2)}, u32[]{:S(2)}) async-start(bf16[32,48,128]{2,1,0:T(8,128)(2,1)} %shard_map.55), calls=%async_computation.3 | async-start | bytes 786432 | tf_op jit(solution)/shard_map/all_to_all | solution.py:291
  65.7 15.6 %collective-permute-start.2 = (bf16[200,128]{1,0:T(8,128)(2,1)S(1)}, bf16[200,128]{1,0:T(8,128)(2,1)S(1)}, u32[]{:S(2)}, u32[]{:S(2)}) collective-permute-start(bf16[200,128]{1,0:T(8,128)(2,1)S(1)} %slice_bitcast_fusion.1), channel_id=1, source_target_pairs={{4,0},{8,4},{12,8},{16,12},{20,16},{24,20},{28,24},{32,28},{36,32}... | collective-permute-start | bytes 153608 | tf_op jit(solution)/shard_map/ppermute | solution.py:287
where the time goes:
time: 83.3 us; the launch traced here: 82.9 us
  blocking collectives  42.3 us (51%)
  starting transfers between devices  19.8 us (24%)
  waiting for transfers between devices  12 us (14%)
  Pallas kernels  7.91 us (9%)
    all_to_all x1, blocking collectives, swap(): return lax.all_to_all(x, axes, split_axis=0, concat_axis=0, tiled=True)  21.1 us
    all_to_all x1, blocking collectives, step(): lax.all_to_all(part, FAR, 0, 0, tiled=True, axis_index_groups=[[4, 5, 6,...  14.8 us
    all_to_all x2, starting transfers between devices, swap(): return lax.all_to_all(x, axes, split_axis=0, concat_axis=0, tiled=True)  14.1 us
    all_to_all x2, waiting for transfers between devices, swap(): return lax.all_to_all(x, axes, split_axis=0, concat_axis=0, tiled=True)  7.86 us
    all_gather x1, blocking collectives, step(): whole = lax.all_gather(part, CORE, axis=0, tiled=True)  6.43 us
    ppermute x1, starting transfers between devices, step(): other = lax.ppermute(terms[1], CORE, [(0, 1), (1, 0)])  3.15 us
    ppermute x2, starting transfers between devices, moved_rows(): return lax.ppermute(x, ROWS, pairs)  2.57 us
    ppermute x2, waiting for transfers between devices, moved_rows(): return lax.ppermute(x, ROWS, pairs)  2.29 us
  transfers between devices with their start and end apart: 5, of which 4 were waited for; matrix products, arithmetic and copies ran while one was open for 0% of the time, Pallas kernels for 2%

commit v1 on v0

--- a/solution.py
+++ b/solution.py
@@ -1,4 +1,5 @@
 import functools
+import itertools
 import math
 
 import jax
@@ -16,6 +17,10 @@
 NEAR = ("r0", "r1", "z0", "c0")
 FAR = "z1"
 CORE = "c1"
+OPEN_COLS = (0, 1)
+OPEN_FIRST = (0, 2, 0, 1)
+OPEN_THIRD = (0, 2, 0, 1)
+OPEN_FAR = (5,)
 BF = jnp.bfloat16
 F32 = jnp.float32
 LANES = 128
@@ -48,7 +53,7 @@
     return jnp.where(q == source, 1.0, 0.0).astype(BF)
 
 
-def send_body(grad_ref, lines_ref, out_ref, row_ref, grad, line, edges, in_sem, out_sem):
+def send_body(order, grad_ref, lines_ref, out_ref, row_ref, grad, line, edges, in_sem, out_sem):
     chans, width = grad_ref.shape
     blocks = out_ref.shape[0]
     block = width // blocks
@@ -64,7 +69,7 @@
     for d in range(blocks):
         puts.append(
             pltpu.make_async_copy(
-                grad.at[:, pl.ds(d * block, block)], out_ref.at[d, pl.ds(0, chans), :], out_sem.at[d]
+                grad.at[:, pl.ds(order[d] * block, block)], out_ref.at[d, pl.ds(0, chans), :], out_sem.at[d]
             )
         )
     puts.append(pltpu.make_async_copy(line, row_ref, out_sem.at[blocks]))
@@ -76,7 +81,8 @@
     take_line.wait()
     puts[blocks].start()
     for d in range(blocks):
-        edges[d] = jnp.concatenate([head[d : d + 1], tail[d : d + 1], jnp.zeros((6, LANES), F32)], axis=0).astype(BF)
+        k = order[d]
+        edges[d] = jnp.concatenate([head[k : k + 1], tail[k : k + 1], jnp.zeros((6, LANES), F32)], axis=0).astype(BF)
     puts.append(pltpu.make_async_copy(edges, out_ref.at[:, pl.ds(chans, 8), :], out_sem.at[blocks + 1]))
     puts[-1].start()
     for put in puts:
@@ -108,12 +114,12 @@
     return jnp.concatenate(rows, axis=0)
 
 
-def filter_body(got_ref, split_ref, above_ref, out_ref, pair_ref):
+def filter_body(order, got_ref, split_ref, above_ref, out_ref, pair_ref):
     rows, chans, width = split_ref.shape
     half = rows // 2
     mine = lax.axis_index(CORE)
     top = mm(above_ref[...], split_matrix(width), NN).astype(BF)
-    blocks = [got_ref[k] for k in range(half)]
+    blocks = [got_ref[order.index(k)] for k in range(half)]
     grads = [b[:chans, :] for b in blocks]
     moved = shifted(grads, edges_of(blocks, chans))
     for k in range(half):
@@ -148,8 +154,11 @@
     put(9 * step, jnp.zeros((TOTAL - 9 * step, LANES), F32))
 
 
-def pair_body(mine_ref, other_ref, out_ref):
-    out_ref[...] = (mine_ref[0] + other_ref[...]).astype(BF)
+def pair_body(sources, mine_ref, other_ref, out_ref):
+    chunk = out_ref.shape[0] // len(sources)
+    for place, source in enumerate(sources):
+        rows = slice(source * chunk, (source + 1) * chunk)
+        out_ref[place * chunk : (place + 1) * chunk, :] = (mine_ref[0, rows, :] + other_ref[rows, :]).astype(BF)
 
 
 def coded(value, top):
@@ -287,8 +296,19 @@
     return lax.ppermute(x, ROWS, pairs)
 
 
-def swap(x, axes):
-    return lax.all_to_all(x, axes, split_axis=0, concat_axis=0, tiled=True)
+def opened(axes, at):
+    sizes = [lax.axis_size(axis) for axis in axes]
+    order = []
+    for place in itertools.product(*(range(size) for size in sizes)):
+        index = 0
+        for step, start, size in zip(place, at, sizes):
+            index = index * size + (step + start) % size
+        order.append(index)
+    return order
+
+
+def swap(x, axes, order):
+    return lax.all_to_all(x, axes, split_axis=0, concat_axis=0, tiled=True, axis_index_groups=[order])
 
 
 def step(grad_out, inputs, weight):
@@ -305,8 +325,11 @@
     stored = pl.BlockSpec(memory_space=pltpu.HBM)
     local = pl.BlockSpec(memory_space=pltpu.VMEM)
     blocks = lax.axis_size(COLS)
+    across = opened(COLS, OPEN_COLS)
+    first = opened(NEAR, OPEN_FIRST)
+    third = opened(NEAR, OPEN_THIRD)
     sent, last = pl.pallas_call(
-        send_body,
+        functools.partial(send_body, across),
         in_specs=[stored, stored],
         out_specs=[stored, stored],
         out_shape=[shape((blocks, chans + 8, LANES), BF), shape((chans, cols), BF)],
@@ -320,12 +343,12 @@
         cost_estimate=pl.CostEstimate(flops=10**8, bytes_accessed=5 * 10**5, transcendentals=0),
         compiler_params=pltpu.CompilerParams(vmem_limit_bytes=63000000),
     )(grad, lines)
-    got = swap(sent, COLS)
+    got = swap(sent, COLS, across)
     above = moved_rows(last, 1)
     split = call(split_body, shape((rows, chans, cols), BF), 2 * 10**8, 2 * 10**6)(lines)
-    below = moved_rows(got[0], -1)
+    below = moved_rows(got[across.index(0)], -1)
     terms, pairs = call(
-        filter_body,
+        functools.partial(filter_body, across),
         (shape((2, own, LANES), F32), shape((half, 2, chans, LANES), BF)),
         10**9,
         4 * 10**6,
@@ -334,12 +357,13 @@
     input_grad, odd_part = call(
         input_body, (shape((rows, chans, cols), BF), shape((2, chans, LANES), F32)), 10**9, 2 * 10**6
     )(pairs, weight)
-    part = call(pair_body, shape((own, LANES), BF), 10**6, 2 * 10**6)(terms, other)
-    part = swap(part.reshape(near, chunk, LANES), NEAR)
+    sources = [third.index(device) for device in first]
+    part = call(functools.partial(pair_body, sources), shape((own, LANES), BF), 10**6, 2 * 10**6)(terms, other)
+    part = swap(part.reshape(near, chunk, LANES), NEAR, first)
     part = call(near_body, shape((far, chunk + 8, LANES), BF), 10**6, 10**6)(part)
-    part = lax.all_to_all(part, FAR, 0, 0, tiled=True, axis_index_groups=[[4, 5, 6, 7, 0, 1, 2, 3]])
+    part = swap(part, FAR, opened((FAR,), OPEN_FAR))
     part = call(far_body, shape((near, chunk, LANES), BF), 10**6, 10**6)(part)
-    part = swap(part, NEAR).reshape(own, LANES)
+    part = swap(part, NEAR, third).reshape(own, LANES)
     whole = lax.all_gather(part, CORE, axis=0, tiled=True)
     filter_grad, input_grad = pl.pallas_call(
         functools.partial(last_body, 1.0 / math.sqrt(positions)),

time: 83.3 us -> 81.7 us (0.981)
  waiting for transfers between devices: 12 us -> 7.34 us
  starting transfers between devices: 19.8 us -> 22 us
    all_to_all x2, waiting for transfers between devices: 7.86 us -> 3.9 us  [swap(): lax.all_to_all(x, axes, split_axis=0, concat_axis=0, tiled=True, axis_ind...]
    all_to_all x2, starting transfers between devices: 14.1 us -> 16.3 us  [swap(): lax.all_to_all(x, axes, split_axis=0, concat_axis=0, tiled=True, axis_ind...]
    all_to_all x2, blocking collectives: 35.9 us -> 37.2 us  [swap(): lax.all_to_all(x, axes, split_axis=0, concat_axis=0, tiled=True, axis_ind...]
    all_gather x1, blocking collectives: 6.43 us -> 5.29 us  [step(): whole = lax.all_gather(part, CORE, axis=0, tiled=True)]
  transfers between devices with their start and end apart: 5 -> 5, of which waited for: 4 -> 4; matrix products, arithmetic and copies ran while one was open for 0% -> 0% of each run, Pallas kernels for 2% -> 3%
where the time goes in v1:
time: 81.7 us; the launch traced here: 80.5 us
  blocking collectives  42.4 us (52%)
  starting transfers between devices  22 us (27%)
  Pallas kernels  7.9 us (10%)
  waiting for transfers between devices  7.34 us (9%)
    all_to_all x2, blocking collectives, swap(): lax.all_to_all(x, axes, split_axis=0, concat_axis=0, tiled=True, axis_ind...  37.2 us
    all_to_all x2, starting transfers between devices, swap(): lax.all_to_all(x, axes, split_axis=0, concat_axis=0, tiled=True, axis_ind...  16.3 us
    all_gather x1, blocking collectives, step(): whole = lax.all_gather(part, CORE, axis=0, tiled=True)  5.29 us
    all_to_all x2, waiting for transfers between devices, swap(): lax.all_to_all(x, axes, split_axis=0, concat_axis=0, tiled=True, axis_ind...  3.9 us
    ppermute x1, starting transfers between devices, step(): other = lax.ppermute(terms[1], CORE, [(0, 1), (1, 0)])  3.15 us
    ppermute x2, starting transfers between devices, moved_rows(): return lax.ppermute(x, ROWS, pairs)  2.57 us
    ppermute x1, waiting for transfers between devices, step(): other = lax.ppermute(terms[1], CORE, [(0, 1), (1, 0)])  1.89 us
    pallas_call x1, Pallas kernels, step(): pl.pallas_call(functools.partial(send_body, across), in_specs=[stored, st...  1.88 us
  transfers between devices with their start and end apart: 5, of which 4 were waited for; matrix products, arithmetic and copies ran while one was open for 0% of the time, Pallas kernels for 3%

profile of v1, /device:TPU:1, one launch (start us, length us, event | category | flops | bytes accessed | tf_op | source)
XLA Modules:
  0.0 80.5 jit_solution(2696517854177783425)
XLA Ops:
  0.6 0.0 copy-start
  0.6 1.9 %shard_map.50 = (bf16[4,200,128]{2,1,0:T(8,128)(2,1)}, bf16[192,256]{1,0:T(8,128)(2,1)}) custom-call(bf16[192,512]{1,0:T(8,128)(2,1)} %bitcast.17, bf16[8,192,256]{2,1,0:T(8,128)(2,1)} %bitcast.12), custom_call_target="tpu_custom_call" | custom-call | flops 100000000 | bytes 500000 | tf_op jit(solution)/shard_map/pallas_call | solution.py:331
  2.5 8.1 %all-to-all-start = ((bf16[4,200,128]{2,1,0:T(8,128)(2,1)}), bf16[4,200,128]{2,1,0:T(8,128)(2,1)S(1)}, u32[]{:S(2)}, u32[]{:S(2)}) async-start(bf16[4,200,128]{2,1,0:T(8,128)(2,1)} %get-tuple-element.10), calls=%async_computation | async-start | bytes 409600 | tf_op jit(solution)/shard_map/all_to_all | solution.py:311
  10.6 1.3 %collective-permute-start = (bf16[192,256]{1,0:T(8,128)(2,1)}, bf16[192,256]{1,0:T(8,128)(2,1)S(1)}, u32[]{:S(2)}, u32[]{:S(2)}) collective-permute-start(bf16[192,256]{1,0:T(8,128)(2,1)} %get-tuple-element.11), channel_id=1, source_target_pairs={{0,4},{4,8},{8,12},{12,16},{16,20},{20,24},{24,28},{28,32},{32,36}... | collective-permute-start | bytes 294920 | tf_op jit(solution)/shard_map/ppermute | solution.py:296
  11.9 0.0 copy-done
  11.9 0.4 shard_map.51.split_ref
  12.3 1.6 %collective-permute-done.above_ref = bf16[192,256]{1,0:T(8,128)(2,1)S(1)} collective-permute-done((bf16[192,256]{1,0:T(8,128)(2,1)}, bf16[192,256]{1,0:T(8,128)(2,1)S(1)}, u32[]{:S(2)}, u32[]{:S(2)}) %collective-permute-start) | collective-permute-done | bytes 98336 | tf_op jit(solution)/shard_map/ppermute | solution.py:296
  13.9 2.5 %all-to-all-done.got_ref = bf16[4,200,128]{2,1,0:T(8,128)(2,1)S(1)} async-done(((bf16[4,200,128]{2,1,0:T(8,128)(2,1)}), bf16[4,200,128]{2,1,0:T(8,128)(2,1)S(1)}, u32[]{:S(2)}, u32[]{:S(2)}) %all-to-all-start) | async-done | bytes 204832 | tf_op jit(solution)/shard_map/all_to_all | solution.py:311
  16.4 1.0 %shard_map.52 = (f32[2,1536,128]{2,1,0:T(8,128)S(1)}, bf16[4,2,192,128]{3,2,1,0:T(8,128)(2,1)S(1)}) custom-call(bf16[4,200,128]{2,1,0:T(8,128)(2,1)S(1)} %all-to-all-done.got_ref, bf16[8,192,256]{2,1,0:T(8,128)(2,1)S(1)} %shard_map.51.split_ref, bf16[192,256]{1,0:T(8,128)(2,1)S(1)} %collective-permute-done.above_ref), custom_call_target="tpu_custom_call" | custom-call | flops 1000000000 | bytes 4000000 | tf_op jit(solution)/shard_map/pallas_call | solution.py:350
  17.4 0.1 slice_bitcast_fusion
  17.4 3.1 %collective-permute-start.1 = (f32[1536,128]{1,0:T(8,128)S(1)}, f32[1536,128]{1,0:T(8,128)S(1)}, u32[]{:S(2)}, u32[]{:S(2)}) collective-permute-start(f32[1536,128]{1,0:T(8,128)S(1)} %slice_bitcast_fusion), channel_id=1, source_target_pairs={{0,1},{1,0},{2,3},{3,2},{4,5},{5,4},{6,7},{7,6},{8,9},{9,8},{10,11... | collective-permute-start | bytes 2359304 | tf_op jit(solution)/shard_map/ppermute | solution.py:356
  20.6 1.9 %collective-permute-done.1.other_ref = f32[1536,128]{1,0:T(8,128)S(1)} collective-permute-done((f32[1536,128]{1,0:T(8,128)S(1)}, f32[1536,128]{1,0:T(8,128)S(1)}, u32[]{:S(2)}, u32[]{:S(2)}) %collective-permute-start.1) | collective-permute-done | bytes 786464 | tf_op jit(solution)/shard_map/ppermute | solution.py:356
  22.5 0.1 shard_map.53
  22.6 0.0 copy-start.1
  22.6 21.2 %all_to_all.20.in_ref = bf16[32,48,128]{2,1,0:T(8,128)(2,1)S(1)} all-to-all(bf16[32,48,128]{2,1,0:T(8,128)(2,1)S(1)} %bitcast.14), channel_id=1, replica_groups={{130,128,134,132,194,192,198,196,2,0,6,4,66,64,70,68,386,384,390,388,45..., dimensions={0} | all-to-all | bytes 786432 | tf_op jit(solution)/shard_map/all_to_all | solution.py:311
  43.8 0.2 shard_map.54
  44.0 15.9 %all_to_all.21.in_ref = bf16[8,56,128]{2,1,0:T(8,128)(2,1)S(1)} all-to-all(bf16[8,56,128]{2,1,0:T(8,128)(2,1)S(1)} %shard_map.54), channel_id=1, replica_groups={{40,48,56,0,8,16,24,32},{41,49,57,1,9,17,25,33},{42,50,58,2,10,18,26,34..., dimensions={0} | all-to-all | bytes 229376 | tf_op jit(solution)/shard_map/all_to_all | solution.py:311
  59.9 1.1 %shard_map.55 = bf16[32,48,128]{2,1,0:T(8,128)(2,1)} custom-call(bf16[8,56,128]{2,1,0:T(8,128)(2,1)S(1)} %all_to_all.21.in_ref), custom_call_target="tpu_custom_call" | custom-call | flops 1000000 | bytes 1000000 | tf_op jit(solution)/shard_map/pallas_call | solution.py:365
  61.0 8.1 %all-to-all-start.3 = ((bf16[32,48,128]{2,1,0:T(8,128)(2,1)}), bf16[32,48,128]{2,1,0:T(8,128)(2,1)S(1)}, u32[]{:S(2)}, u32[]{:S(2)}) async-start(bf16[32,48,128]{2,1,0:T(8,128)(2,1)} %shard_map.55), calls=%async_computation.3 | async-start | bytes 786432 | tf_op jit(solution)/shard_map/all_to_all | solution.py:311
  69.2 1.3 %collective-permute-start.2 = (bf16[200,128]{1,0:T(8,128)(2,1)S(1)}, bf16[200,128]{1,0:T(8,128)(2,1)S(1)}, u32[]{:S(2)}, u32[]{:S(2)}) collective-permute-start(bf16[200,128]{1,0:T(8,128)(2,1)S(1)} %slice_bitcast_fusion.1), channel_id=1, source_target_pairs={{4,0},{8,4},{12,8},{16,12},{20,16},{24,20},{28,24},{32,28},{36,32}... | collective-permute-start | bytes 153608 | tf_op jit(solution)/shard_map/ppermute | solution.py:296
  70.5 0.0 copy-done.1
  70.5 1.7 %shard_map.56 = (bf16[8,192,256]{2,1,0:T(8,128)(2,1)}, f32[2,192,128]{2,1,0:T(8,128)S(1)}) custom-call(bf16[4,2,192,128]{3,2,1,0:T(8,128)(2,1)S(1)} %get-tuple-element.13.pair_ref, bf16[3,3,192,192]{3,2,1,0:T(8,128)(2,1)S(1)} %copy-done.1), custom_call_target="tpu_custom_call" | custom-call | flops 1000000000 | bytes 2000000 | tf_op jit(solution)/shard_map/pallas_call | solution.py:357
  72.2 1.3 %all-to-all-done.3 = bf16[32,48,128]{2,1,0:T(8,128)(2,1)S(1)} async-done(((bf16[32,48,128]{2,1,0:T(8,128)(2,1)}), bf16[32,48,128]{2,1,0:T(8,128)(2,1)S(1)}, u32[]{:S(2)}, u32[]{:S(2)}) %all-to-all-start.3) | async-done | bytes 393248 | tf_op jit(solution)/shard_map/all_to_all | solution.py:311
  73.6 5.3 %all_gather.3.in_ref = bf16[3072,128]{1,0:T(8,128)(2,1)S(1)} all-gather(bf16[1536,128]{1,0:T(8,128)(2,1)S(1)} %bitcast.15), channel_id=1, replica_groups=mesh['r0'=2,'r1'=4,'z1'=8,'z0'=2,'c0'=2,'c1'=2] {'c1'}, dimensions={0}, use_global_device_ids=true | all-gather | bytes 1179648 | tf_op jit(solution)/shard_map/all_gather | solution.py:367
  78.9 0.0 collective-permute-done.2.below_ref
  78.9 1.6 %shard_map.57 = (f32[9,192,192]{2,1,0:T(8,128)}, bf16[8,192,256]{2,1,0:T(8,128)(2,1)}) custom-call(bf16[3072,128]{1,0:T(8,128)(2,1)S(1)} %all_gather.3.in_ref, bf16[200,128]{1,0:T(8,128)(2,1)S(1)} %collective-permute-done.2.below_ref, bf16[3,3,192,192]{3,2,1,0:T(8,128)(2,1)S(1)} %copy-done.1, ...), custom_call_target="tpu_custom_call", output_to_operand_aliasing={{1}: (4, {})} | custom-call | flops 1000000 | bytes 2000000 | tf_op jit(solution)/shard_map/pallas_call | solution.py:368
  (1 shorter events, 0.0 us)
Async XLA Ops:
  0.6 11.3 %copy-start = (bf16[8,256,192]{1,2,0:T(8,128)(2,1)S(1)}, bf16[8,256,192]{1,2,0:T(8,128)(2,1)}, u32[]{:S(2)}) copy-start(bf16[8,256,192]{1,2,0:T(8,128)(2,1)} %param.4) | copy-start | bytes 2359300
  2.5 13.9 %all-to-all-start = ((bf16[4,200,128]{2,1,0:T(8,128)(2,1)}), bf16[4,200,128]{2,1,0:T(8,128)(2,1)S(1)}, u32[]{:S(2)}, u32[]{:S(2)}) async-start(bf16[4,200,128]{2,1,0:T(8,128)(2,1)} %get-tuple-element.10), calls=%async_computation | async-start | bytes 409600 | tf_op jit(solution)/shard_map/all_to_all | solution.py:311
  10.6 3.2 %collective-permute-start = (bf16[192,256]{1,0:T(8,128)(2,1)}, bf16[192,256]{1,0:T(8,128)(2,1)S(1)}, u32[]{:S(2)}, u32[]{:S(2)}) collective-permute-start(bf16[192,256]{1,0:T(8,128)(2,1)} %get-tuple-element.11), channel_id=1, source_target_pairs={{0,4},{4,8},{8,12},{12,16},{16,20},{20,24},{24,28},{28,32},{32,36}... | collective-permute-start | bytes 294920 | tf_op jit(solution)/shard_map/ppermute | solution.py:296
  17.4 5.0 %collective-permute-start.1 = (f32[1536,128]{1,0:T(8,128)S(1)}, f32[1536,128]{1,0:T(8,128)S(1)}, u32[]{:S(2)}, u32[]{:S(2)}) collective-permute-start(f32[1536,128]{1,0:T(8,128)S(1)} %slice_bitcast_fusion), channel_id=1, source_target_pairs={{0,1},{1,0},{2,3},{3,2},{4,5},{5,4},{6,7},{7,6},{8,9},{9,8},{10,11... | collective-permute-start | bytes 2359304 | tf_op jit(solution)/shard_map/ppermute | solution.py:356
  22.6 47.9 %copy-start.1 = (bf16[3,3,192,192]{3,2,1,0:T(8,128)(2,1)S(1)}, bf16[3,3,192,192]{3,2,1,0:T(8,128)(2,1)}, u32[]{:S(2)}) copy-start(bf16[3,3,192,192]{3,2,1,0:T(8,128)(2,1)} %weight_ref.3) | copy-start | bytes 1990660
  61.0 12.5 %all-to-all-start.3 = ((bf16[32,48,128]{2,1,0:T(8,128)(2,1)}), bf16[32,48,128]{2,1,0:T(8,128)(2,1)S(1)}, u32[]{:S(2)}, u32[]{:S(2)}) async-start(bf16[32,48,128]{2,1,0:T(8,128)(2,1)} %shard_map.55), calls=%async_computation.3 | async-start | bytes 786432 | tf_op jit(solution)/shard_map/all_to_all | solution.py:311
  69.2 9.6 %collective-permute-start.2 = (bf16[200,128]{1,0:T(8,128)(2,1)S(1)}, bf16[200,128]{1,0:T(8,128)(2,1)S(1)}, u32[]{:S(2)}, u32[]{:S(2)}) collective-permute-start(bf16[200,128]{1,0:T(8,128)(2,1)S(1)} %slice_bitcast_fusion.1), channel_id=1, source_target_pairs={{4,0},{8,4},{12,8},{16,12},{20,16},{24,20},{28,24},{32,28},{36,32}... | collective-permute-start | bytes 153608 | tf_op jit(solution)/shard_map/ppermute | solution.py:296
